TPU v7x, 128 devices: a whole 4x4x4 slice. The times are simulated.
128 devices in a mesh: grp: 8 (over z, core), col: 16 (over x, y).
Axes of the slice: x: 4, y: 4, z: 4, core: 2. Of those that a mesh axis runs over, the one named last changes fastest.
Arguments:
- x_blocks: bfloat16 [32, 16, 6, 256, 256], P('grp', 'col'), may hold values from -6 to 6
- columns: int32 [32, 16, 6], replicated, may hold values from -1 to 511, as said below
- filter_ids: int32 [32, 16, 6], replicated, may hold values from 0 to 511, as said below
Outputs:
- sign_step: bfloat16 [32, 16, 6, 256, 256], P('grp', 'col')
Inputs may be any that keep to these rules, and one draw needn't show every extreme that they name: `columns`: in each block row of the grid, slot 0 holds the row's own id; the other used slots hold distinct ids of block rows at most one step away along each grid dimension, with periodic wrap; used slots come first, then -1; at least 3 slots are used. `filter_ids`: in each block row, slot 0 holds the row's own id and the others distinct ids of block rows at most one step away along each grid dimension, with periodic wrap.
All inputs are finite; a program needn't handle non-finite values.
Results may differ from a plain program's by a relative error of at most 0.0019.
Values may be sent and summed in bfloat16 or wider, within the bound.
A program may use at most 128 MiB of HBM per device.

v0:
```python
import jax
import jax.numpy as jnp
from jax import lax
from jax.sharding import PartitionSpec as P

B = 256
KB = 6
KF = 6


def padded(cells, sides, width):
    for axis, dim in sides:
        count = lax.axis_size(axis)
        head = lax.slice_in_dim(cells, 0, width, axis=dim)
        tail = lax.slice_in_dim(cells, cells.shape[dim] - width, cells.shape[dim], axis=dim)
        cells = jnp.concatenate(
            [
                lax.ppermute(tail, axis, [(i, (i + 1) % count) for i in range(count)]),
                cells,
                lax.ppermute(head, axis, [((i + 1) % count, i) for i in range(count)]),
            ],
            axis=dim,
        )
    return cells


def block_terms(
    halo, pos_a, pos_c, row_ids, row_cols, left_blocks, stored_table, wanted, grid_a, grid_c
):
    slot_count = halo.shape[2]
    width = halo.shape[3]
    in_use = row_cols >= 0
    source = jnp.where(in_use, row_cols, 0)
    home_a = row_ids // grid_c
    home_c = row_ids % grid_c
    step_a = (source // grid_c - home_a[:, None] + 1) % grid_a - 1
    step_c = (source % grid_c - home_c[:, None] + 1) % grid_c - 1
    place = (pos_a[:, None] + step_a) * halo.shape[1] + pos_c[:, None] + step_c
    flat = halo.reshape((halo.shape[0] * halo.shape[1] * slot_count, width, width))
    stored = stored_table[source]
    matches = stored[:, :, None, :] == wanted[:, None, :, None]
    present = jnp.any(matches, axis=3) & (wanted[:, None, :] >= 0) & in_use[:, :, None]
    slot_of = jnp.argmax(matches.astype(jnp.int32), axis=3)
    block_index = place[:, :, None] * slot_count + slot_of

    def one_row(inputs):
        index_row, present_row, left_row = inputs
        picked = flat[index_row]
        picked = jnp.where(present_row[:, :, None, None], picked, jnp.zeros((), picked.dtype))
        return jnp.einsum("kab,kfbc->fac", left_row, picked, preferred_element_type=jnp.float32)

    return lax.map(one_row, (block_index, present, left_blocks))


def local(x_blocks, columns, filter_ids):
    grp_count = lax.axis_size("grp")
    col_count = lax.axis_size("col")
    rows_a = x_blocks.shape[0]
    rows_c = x_blocks.shape[1]
    grid_a = rows_a * grp_count
    grid_c = rows_c * col_count
    col_table = columns.reshape(grid_a * grid_c, KB)
    filt_table = filter_ids.reshape(grid_a * grid_c, KF)
    local_rows = rows_a * rows_c
    offsets = jnp.arange(local_rows, dtype=jnp.int32)
    local_a = offsets // rows_c
    local_c = offsets % rows_c
    row_ids = (
        (lax.axis_index("grp") * rows_a + local_a) * grid_c
        + lax.axis_index("col") * rows_c
        + local_c
    )
    row_cols = col_table[row_ids]
    left_blocks = x_blocks.reshape(local_rows, KB, B, B)
    along_col = padded(x_blocks, (("col", 1),), 1)
    near_x = padded(along_col, (("grp", 0),), 1)
    square = block_terms(
        near_x,
        local_a + 1,
        local_c + 1,
        row_ids,
        row_cols,
        left_blocks,
        col_table,
        filt_table[row_ids],
        grid_a,
        grid_c,
    ).astype(jnp.bfloat16)
    square = square.reshape(rows_a, rows_c, KF, B, B)
    square_along = padded(square, (("col", 1),), 1)
    near_square = padded(square_along, (("grp", 0),), 1)
    cubed = block_terms(
        near_square,
        local_a + 1,
        local_c + 1,
        row_ids,
        row_cols,
        left_blocks,
        filt_table,
        row_cols,
        grid_a,
        grid_c,
    )
    in_use = (row_cols >= 0).astype(jnp.float32)
    result = (1.5 * left_blocks.astype(jnp.float32) - cubed * (0.5 / (KB * B))) * in_use[
        :, :, None, None
    ]
    return result.astype(jnp.bfloat16).reshape(x_blocks.shape)


def solution(mesh):
    return jax.shard_map(
        local,
        mesh=mesh,
        in_specs=(P("grp", "col", None, None, None), P(), P()),
        out_specs=P("grp", "col", None, None, None),
        check_vma=False,
    )
```

profile of v0, /device:TPU:1, one launch (start us, length us, event | category | flops | bytes accessed | tf_op | source)
XLA Modules:
  0.0 435.9 jit_solution(5830552396138790806)
XLA Ops:
  0.0 2.1 collective-permute-start
  2.1 3.7 collective-permute-start.1
  6.8 67.1 %collective-permute-done = bf16[4,1,6,256,256]{4,3,2,1,0:T(8,128)(2,1)} collective-permute-done((bf16[4,1,6,256,256]{4,3,2,1,0:T(8,128)(2,1)}, bf16[4,1,6,256,256]{4,3,2,1,0:T(8,128)(2,1)}, u32[]{:S(2)}, u32[]{:S(2)}) %collective-permute-start) | collective-permute-done | bytes 3145760 | tf_op jit(solution)/shard_map/ppermute | solution.py:18
  73.9 2.1 constant_dynamic-update-slice_fusion.3
  76.3 2.1 constant_dynamic-update-slice_fusion.1
  78.4 2.7 fusion.42
  81.1 2.2 copy-done
  83.4 2.8 collective-permute-start.2
  89.2 1.4 compare_reduce_fusion
  91.0 2.0 fusion.24
  92.9 2.0 fusion.25
  95.0 17.2 %collective-permute-done.2 = bf16[1,3,6,256,256]{4,3,2,1,0:T(8,128)(2,1)} collective-permute-done((bf16[1,3,6,256,256]{4,3,2,1,0:T(8,128)(2,1)}, bf16[1,3,6,256,256]{4,3,2,1,0:T(8,128)(2,1)}, u32[]{:S(2)}, u32[]{:S(2)}) %collective-permute-start.2) | collective-permute-done | bytes 2359328 | tf_op jit(solution)/shard_map/ppermute | solution.py:18
  112.3 2.5 collective-permute-done.3
  114.7 10.6 %pad_maximum_fusion = bf16[6,3,6,256,256]{4,3,2,1,0:T(8,128)(2,1)} fusion(bf16[1,3,6,256,256]{4,3,2,1,0:T(8,128)(2,1)} %collective-permute-done.3, bf16[4,3,6,256,256]{4,3,2,1,0:T(8,128)(2,1)} %copy-done, bf16[1,3,6,256,256]{4,3,2,1,0:T(8,128)(2,1)} %collective-permute-done.2), kind=kLoop, calls=%fused_computation.33 | loop fusion | flops 14155776 | bytes 28311552 | tf_op jit(solution)/shard_map/concatenate | solution.py:16
  125.3 81.1 %while.20 = (s32[]{:T(128)}, bf16[4,6,256,256]{2,3,1,0:T(8,128)(2,1)S(1)}, pred[4,6,6]{2,1,0:T(8,128)(4,1)S(1)}, s32[4,6,6]{2,0,1:T(4,128)S(1)}, bf16[108,256,25...) while((s32[]{:T(128)}, bf16[4,6,256,256]{2,3,1,0:T(8,128)(2,1)S(1)}, ...), condition=%wide.region_5.6_spmd, body=%wide.region_4.5_spmd.sunk | while | flops 1210320000 | bytes 25959492 | solution.py:52
  125.4 9.4 %gather_fusion = bf16[36,256,256]{2,1,0:T(8,128)(2,1)} fusion(bf16[108,256,256]{2,1,0:T(8,128)(2,1)} %get-tuple-element.217, s32[1024]{0:T(1024)S(1)} %pad_clamp_fusion.6), kind=kCustom, calls=%fused_computation.clone.1 | custom fusion | bytes 9437328 | tf_op jit(solution)/shard_map/while/body/eval_jaxpr/gather | solution.py:48
  134.9 6.6 %copy.65 = bf16[6,6,256,256]{2,3,0,1:T(8,128)(2,1)} copy(bf16[6,6,256,256]{3,2,1,0:T(8,128)(2,1)} %bitcast.69) | data formatting | bytes 9437184 | tf_op jit(solution)/shard_map/while/body/eval_jaxpr/gather | solution.py:48
  141.6 4.0 bitcast_dynamic-update-slice_fusion.2
  145.8 9.3 %gather_fusion = bf16[36,256,256]{2,1,0:T(8,128)(2,1)} fusion(bf16[108,256,256]{2,1,0:T(8,128)(2,1)} %get-tuple-element.217, s32[1024]{0:T(1024)S(1)} %pad_clamp_fusion.6), kind=kCustom, calls=%fused_computation.clone.1 | custom fusion | bytes 9437328 | tf_op jit(solution)/shard_map/while/body/eval_jaxpr/gather | solution.py:48
  155.1 6.6 %copy.65 = bf16[6,6,256,256]{2,3,0,1:T(8,128)(2,1)} copy(bf16[6,6,256,256]{3,2,1,0:T(8,128)(2,1)} %bitcast.69) | data formatting | bytes 9437184 | tf_op jit(solution)/shard_map/while/body/eval_jaxpr/gather | solution.py:48
  161.9 4.0 bitcast_dynamic-update-slice_fusion.2
  166.0 9.3 %gather_fusion = bf16[36,256,256]{2,1,0:T(8,128)(2,1)} fusion(bf16[108,256,256]{2,1,0:T(8,128)(2,1)} %get-tuple-element.217, s32[1024]{0:T(1024)S(1)} %pad_clamp_fusion.6), kind=kCustom, calls=%fused_computation.clone.1 | custom fusion | bytes 9437328 | tf_op jit(solution)/shard_map/while/body/eval_jaxpr/gather | solution.py:48
  175.3 6.6 %copy.65 = bf16[6,6,256,256]{2,3,0,1:T(8,128)(2,1)} copy(bf16[6,6,256,256]{3,2,1,0:T(8,128)(2,1)} %bitcast.69) | data formatting | bytes 9437184 | tf_op jit(solution)/shard_map/while/body/eval_jaxpr/gather | solution.py:48
  182.1 4.0 bitcast_dynamic-update-slice_fusion.2
  186.2 9.5 %gather_fusion = bf16[36,256,256]{2,1,0:T(8,128)(2,1)} fusion(bf16[108,256,256]{2,1,0:T(8,128)(2,1)} %get-tuple-element.217, s32[1024]{0:T(1024)S(1)} %pad_clamp_fusion.6), kind=kCustom, calls=%fused_computation.clone.1 | custom fusion | bytes 9437328 | tf_op jit(solution)/shard_map/while/body/eval_jaxpr/gather | solution.py:48
  195.7 6.6 %copy.65 = bf16[6,6,256,256]{2,3,0,1:T(8,128)(2,1)} copy(bf16[6,6,256,256]{3,2,1,0:T(8,128)(2,1)} %bitcast.69) | data formatting | bytes 9437184 | tf_op jit(solution)/shard_map/while/body/eval_jaxpr/gather | solution.py:48
  202.4 4.0 bitcast_dynamic-update-slice_fusion.2
  206.5 4.8 %collective-permute-start.5 = (bf16[4,1,6,256,256]{3,4,2,0,1:T(8,128)(2,1)S(1)}, bf16[4,1,6,256,256]{3,4,2,0,1:T(8,128)(2,1)S(1)}, u32[]{:S(2)}, u32[]{:S(2)}) collective-permute-start(bf16[4,1,6,256,256]{3,4,2,0,1:T(8,128)(2,1)S(1)} %bitcast.74), channel_id=1, source_target_pairs={{1,0},{2,1},{3,2},{4,3},{5,4},{6,5},{7,6},{8,7},{9,8},{10,9},{11,1... | collective-permute-start | bytes 9437192 | tf_op jit(solution)/shard_map/ppermute | solution.py:20
  211.3 68.4 %collective-permute-done.4 = bf16[4,1,6,256,256]{3,4,2,0,1:T(8,128)(2,1)S(1)} collective-permute-done((bf16[4,1,6,256,256]{3,4,2,0,1:T(8,128)(2,1)S(1)}, bf16[4,1,6,256,256]{3,4,2,0,1:T(8,128)(2,1)S(1)}, u32[]{:S(2)}, u32[]{:S(2)}) %collective-permute-start.4) | collective-permute-done | bytes 3145760 | tf_op jit(solution)/shard_map/ppermute | solution.py:18
  279.7 2.6 pad_maximum_fusion.4
  284.7 25.2 %collective-permute-done.6 = bf16[1,3,6,256,256]{3,4,2,0,1:T(8,128)(2,1)} collective-permute-done((bf16[1,3,6,256,256]{3,4,2,0,1:T(8,128)(2,1)}, bf16[1,3,6,256,256]{3,4,2,0,1:T(8,128)(2,1)}, u32[]{:S(2)}, u32[]{:S(2)}) %collective-permute-start.6) | collective-permute-done | bytes 2359328 | tf_op jit(solution)/shard_map/ppermute | solution.py:18
  309.9 2.8 collective-permute-done.7
  312.7 10.0 %pad_maximum_fusion.1 = bf16[6,3,6,256,256]{3,4,2,0,1:T(8,128)(2,1)} fusion(bf16[1,3,6,256,256]{3,4,2,0,1:T(8,128)(2,1)} %collective-permute-done.7, bf16[4,1,6,256,256]{3,4,2,0,1:T(8,128)(2,1)} %copy-done.2, bf16[4,1,6,256,256]{3,4,2,0,1:T(8,128)(2,1)S(1)} %bitcast.76, bf16[4,1,6,256,256]{3,4,2,0,1:T(8,128)(2,1)} %copy-done.1, ...), kind=kLoop, calls=%fused_computation.34 | loop fusion | flops 28311552 | bytes 28311552 | tf_op jit(solution)/shard_map/concatenate | solution.py:16
  322.6 18.6 %copy.48 = bf16[6,3,6,256,256]{4,3,2,1,0:T(8,128)(2,1)} copy(bf16[6,3,6,256,256]{3,4,2,0,1:T(8,128)(2,1)} %pad_maximum_fusion.1) | data formatting | bytes 28311552 | tf_op jit(solution)/shard_map/concatenate | solution.py:16
  341.2 88.0 %while.21 = (s32[]{:T(128)}, f32[4,6,256,256]{3,2,1,0:T(8,128)}, pred[4,6,6]{2,1,0:T(8,128)(4,1)S(1)}, s32[4,6,6]{2,0,1:T(4,128)S(1)}, bf16[108,256,256]{2,1,0:T...) while((s32[]{:T(128)}, f32[4,6,256,256]{3,2,1,0:T(8,128)}, pred[4,6,6]{2,1,0:T(8,128)(4,1)S(1)}, ...), condition=%wide.region_7.8_spmd, body=%wide.region_6.7_spmd.sunk | while | flops 1210320000 | bytes 32249960 | solution.py:52
  341.3 9.4 %gather_fusion.1 = bf16[36,256,256]{2,1,0:T(8,128)(2,1)} fusion(bf16[108,256,256]{2,1,0:T(8,128)(2,1)} %get-tuple-element.238, s32[1024]{0:T(1024)S(1)} %pad_clamp_fusion.7), kind=kCustom, calls=%fused_computation.1.clone.1 | custom fusion | bytes 9437328 | tf_op jit(solution)/shard_map/while/body/eval_jaxpr/gather | solution.py:48
  350.8 6.6 %copy.67 = bf16[6,6,256,256]{2,3,0,1:T(8,128)(2,1)} copy(bf16[6,6,256,256]{3,2,1,0:T(8,128)(2,1)} %bitcast.70) | data formatting | bytes 9437184 | tf_op jit(solution)/shard_map/while/body/eval_jaxpr/gather | solution.py:48
  357.5 4.0 fusion.56
  363.4 9.3 %gather_fusion.1 = bf16[36,256,256]{2,1,0:T(8,128)(2,1)} fusion(bf16[108,256,256]{2,1,0:T(8,128)(2,1)} %get-tuple-element.238, s32[1024]{0:T(1024)S(1)} %pad_clamp_fusion.7), kind=kCustom, calls=%fused_computation.1.clone.1 | custom fusion | bytes 9437328 | tf_op jit(solution)/shard_map/while/body/eval_jaxpr/gather | solution.py:48
  372.8 6.6 %copy.67 = bf16[6,6,256,256]{2,3,0,1:T(8,128)(2,1)} copy(bf16[6,6,256,256]{3,2,1,0:T(8,128)(2,1)} %bitcast.70) | data formatting | bytes 9437184 | tf_op jit(solution)/shard_map/while/body/eval_jaxpr/gather | solution.py:48
  379.5 4.0 fusion.56
  385.4 9.3 %gather_fusion.1 = bf16[36,256,256]{2,1,0:T(8,128)(2,1)} fusion(bf16[108,256,256]{2,1,0:T(8,128)(2,1)} %get-tuple-element.238, s32[1024]{0:T(1024)S(1)} %pad_clamp_fusion.7), kind=kCustom, calls=%fused_computation.1.clone.1 | custom fusion | bytes 9437328 | tf_op jit(solution)/shard_map/while/body/eval_jaxpr/gather | solution.py:48
  394.7 6.6 %copy.67 = bf16[6,6,256,256]{2,3,0,1:T(8,128)(2,1)} copy(bf16[6,6,256,256]{3,2,1,0:T(8,128)(2,1)} %bitcast.70) | data formatting | bytes 9437184 | tf_op jit(solution)/shard_map/while/body/eval_jaxpr/gather | solution.py:48
  401.4 4.0 fusion.56
  407.3 9.5 %gather_fusion.1 = bf16[36,256,256]{2,1,0:T(8,128)(2,1)} fusion(bf16[108,256,256]{2,1,0:T(8,128)(2,1)} %get-tuple-element.238, s32[1024]{0:T(1024)S(1)} %pad_clamp_fusion.7), kind=kCustom, calls=%fused_computation.1.clone.1 | custom fusion | bytes 9437328 | tf_op jit(solution)/shard_map/while/body/eval_jaxpr/gather | solution.py:48
  416.8 6.6 %copy.67 = bf16[6,6,256,256]{2,3,0,1:T(8,128)(2,1)} copy(bf16[6,6,256,256]{3,2,1,0:T(8,128)(2,1)} %bitcast.70) | data formatting | bytes 9437184 | tf_op jit(solution)/shard_map/while/body/eval_jaxpr/gather | solution.py:48
  423.5 4.0 fusion.56
  429.3 6.6 %fusion.23 = bf16[4,1,6,256,256]{4,3,2,1,0:T(8,128)(2,1)} fusion(f32[4,6,256,256]{3,2,1,0:T(8,128)} %get-tuple-element.74, f32[4,6]{1,0:T(4,128)S(1)} %get-tuple-element.111, bf16[4,1,6,256,256]{4,3,2,1,0:T(8,128)(2,1)} %bitcast.78), kind=kLoop, calls=%fused_computation.36 | loop fusion | flops 9437184 | bytes 12583008 | tf_op jit(solution)/shard_map/reshape | solution.py:108
  (97 shorter events, 15.9 us)
Async XLA Ops:
  0.0 76.0 %copy-start.3 = (bf16[4,1,6,256,256]{4,3,2,1,0:T(8,128)(2,1)S(1)}, bf16[4,1,6,256,256]{4,3,2,1,0:T(8,128)(2,1)}, u32[]{:S(2)}) copy-start(bf16[4,1,6,256,256]{4,3,2,1,0:T(8,128)(2,1)} %param.7) | copy-start | bytes 9437188
  0.0 73.9 %collective-permute-start = (bf16[4,1,6,256,256]{4,3,2,1,0:T(8,128)(2,1)}, bf16[4,1,6,256,256]{4,3,2,1,0:T(8,128)(2,1)}, u32[]{:S(2)}, u32[]{:S(2)}) collective-permute-start(bf16[4,1,6,256,256]{4,3,2,1,0:T(8,128)(2,1)} %param.7), channel_id=1, source_target_pairs={{0,1},{1,2},{2,3},{3,4},{4,5},{5,6},{6,7},{7,8},{8,9},{9,10},{10,1... | collective-permute-start | bytes 9437192 | tf_op jit(solution)/shard_map/ppermute | solution.py:18
  2.1 74.2 %collective-permute-start.1 = (bf16[4,1,6,256,256]{4,3,2,1,0:T(8,128)(2,1)}, bf16[4,1,6,256,256]{4,3,2,1,0:T(8,128)(2,1)}, u32[]{:S(2)}, u32[]{:S(2)}) collective-permute-start(bf16[4,1,6,256,256]{4,3,2,1,0:T(8,128)(2,1)} %param.7), channel_id=1, source_target_pairs={{1,0},{2,1},{3,2},{4,3},{5,4},{6,5},{7,6},{8,7},{9,8},{10,9},{11,1... | collective-permute-start | bytes 9437192 | tf_op jit(solution)/shard_map/ppermute | solution.py:20
  78.4 5.0 %copy-start = (bf16[4,3,6,256,256]{4,3,2,1,0:T(8,128)(2,1)}, bf16[4,3,6,256,256]{4,3,2,1,0:T(8,128)(2,1)S(1)}, u32[]{:S(2)}) copy-start(bf16[4,3,6,256,256]{4,3,2,1,0:T(8,128)(2,1)S(1)} %constant_dynamic-update-slice_fusion.1) | copy-start | bytes 28311556
  78.4 8.5 %copy-start.4 = (s32[32,16,6]{0,1,2:T(8,128)S(1)}, s32[32,16,6]{0,1,2:T(8,128)}, u32[]{:S(2)}) copy-start(s32[32,16,6]{0,1,2:T(8,128)} %param.9) | copy-start | bytes 36868
  83.4 28.9 %collective-permute-start.2 = (bf16[1,3,6,256,256]{4,3,2,1,0:T(8,128)(2,1)}, bf16[1,3,6,256,256]{4,3,2,1,0:T(8,128)(2,1)}, u32[]{:S(2)}, u32[]{:S(2)}) collective-permute-start(bf16[1,3,6,256,256]{4,3,2,1,0:T(8,128)(2,1)} %get-tuple-element.115), channel_id=1, source_target_pairs={{0,16},{16,32},{32,48},{48,64},{64,80},{80,96},{96,112},{112,0},{1... | collective-permute-start | bytes 7077896 | tf_op jit(solution)/shard_map/ppermute | solution.py:18
  86.1 28.6 %collective-permute-start.3 = (bf16[1,3,6,256,256]{4,3,2,1,0:T(8,128)(2,1)}, bf16[1,3,6,256,256]{4,3,2,1,0:T(8,128)(2,1)}, u32[]{:S(2)}, u32[]{:S(2)}) collective-permute-start(bf16[1,3,6,256,256]{4,3,2,1,0:T(8,128)(2,1)} %get-tuple-element.116), channel_id=1, source_target_pairs={{16,0},{32,16},{48,32},{64,48},{80,64},{96,80},{112,96},{0,112},{1... | collective-permute-start | bytes 7077896 | tf_op jit(solution)/shard_map/ppermute | solution.py:20
  206.4 73.2 %collective-permute-start.4 = (bf16[4,1,6,256,256]{3,4,2,0,1:T(8,128)(2,1)S(1)}, bf16[4,1,6,256,256]{3,4,2,0,1:T(8,128)(2,1)S(1)}, u32[]{:S(2)}, u32[]{:S(2)}) collective-permute-start(bf16[4,1,6,256,256]{3,4,2,0,1:T(8,128)(2,1)S(1)} %bitcast.73), channel_id=1, source_target_pairs={{0,1},{1,2},{2,3},{3,4},{4,5},{5,6},{6,7},{7,8},{8,9},{9,10},{10,1... | collective-permute-start | bytes 9437192 | tf_op jit(solution)/shard_map/ppermute | solution.py:18
  206.5 73.2 %collective-permute-start.5 = (bf16[4,1,6,256,256]{3,4,2,0,1:T(8,128)(2,1)S(1)}, bf16[4,1,6,256,256]{3,4,2,0,1:T(8,128)(2,1)S(1)}, u32[]{:S(2)}, u32[]{:S(2)}) collective-permute-start(bf16[4,1,6,256,256]{3,4,2,0,1:T(8,128)(2,1)S(1)} %bitcast.74), channel_id=1, source_target_pairs={{1,0},{2,1},{3,2},{4,3},{5,4},{6,5},{7,6},{8,7},{9,8},{10,9},{11,1... | collective-permute-start | bytes 9437192 | tf_op jit(solution)/shard_map/ppermute | solution.py:20
  279.7 3.1 copy-start.1
  279.7 4.1 copy-start.2
  283.8 26.1 %collective-permute-start.6 = (bf16[1,3,6,256,256]{3,4,2,0,1:T(8,128)(2,1)}, bf16[1,3,6,256,256]{3,4,2,0,1:T(8,128)(2,1)}, u32[]{:S(2)}, u32[]{:S(2)}) collective-permute-start(bf16[1,3,6,256,256]{3,4,2,0,1:T(8,128)(2,1)} %get-tuple-element.113), channel_id=1, source_target_pairs={{0,16},{16,32},{32,48},{48,64},{64,80},{80,96},{96,112},{112,0},{1... | collective-permute-start | bytes 7077896 | tf_op jit(solution)/shard_map/ppermute | solution.py:18
  283.8 28.9 %collective-permute-start.7 = (bf16[1,3,6,256,256]{3,4,2,0,1:T(8,128)(2,1)}, bf16[1,3,6,256,256]{3,4,2,0,1:T(8,128)(2,1)}, u32[]{:S(2)}, u32[]{:S(2)}) collective-permute-start(bf16[1,3,6,256,256]{3,4,2,0,1:T(8,128)(2,1)} %get-tuple-element.114), channel_id=1, source_target_pairs={{16,0},{32,16},{48,32},{64,48},{80,64},{96,80},{112,96},{0,112},{1... | collective-permute-start | bytes 7077896 | tf_op jit(solution)/shard_map/ppermute | solution.py:20
where the time goes:
time: 438 us; the launch traced here: 436 us
  waiting for transfers between devices  183 us (42%)
  local copies, waits for them, and re-layouts  171 us (39%)
  other arithmetic  35.5 us (8%)
  matrix products  31.9 us (7%)
  starting transfers between devices  14.1 us (3%)
    ppermute x4, waiting for transfers between devices, padded(): lax.ppermute(tail, axis, [(i, (i + 1) % count) for i in range(count)])  178 us
    gather x16, local copies, waits for them, and re-layouts, one_row(): picked = flat[index_row]  128 us
    dot_general x8, matrix products, one_row(): jnp.einsum('kab,kfbc->fac', left_row, picked, preferred_element_type=jnp....  31.9 us
    concatenate x2, local copies, waits for them, and re-layouts, padded(): jnp.concatenate([lax.ppermute(tail, axis, [(i, (i + 1) % count) for i in...  20.7 us
    concatenate x2, other arithmetic, padded(): jnp.concatenate([lax.ppermute(tail, axis, [(i, (i + 1) % count) for i in...  20.6 us
    ppermute x4, starting transfers between devices, padded(): lax.ppermute(head, axis, [((i + 1) % count, i) for i in range(count)])  9.11 us
  transfers between devices with their start and end apart: 8, of which 6 were waited for; matrix products, arithmetic and copies ran while one was open for 3% of the time, Pallas kernels for 0%

commit v1 on v0

--- a/solution.py
+++ b/solution.py
@@ -1,11 +1,25 @@
+import functools
+
 import jax
 import jax.numpy as jnp
 from jax import lax
+from jax.experimental import pallas as pl
+from jax.experimental.pallas import tpu as pltpu
 from jax.sharding import PartitionSpec as P
 
 B = 256
 KB = 6
 KF = 6
+RA = 4
+OWN = RA * KB
+CR = 2 * RA + 2
+COLN = CR * KB
+ZERO = COLN
+FIRST = 5
+LEVELS = ((13, 16), (16, 20))
+
+SRC1, SRC2, PICK1, PICK2, USED = 0, 64, 128, 272, 416
+MESH = pl.DeviceIdType.MESH
 
 
 def padded(cells, sides, width):
@@ -52,7 +66,7 @@
     return lax.map(one_row, (block_index, present, left_blocks))
 
 
-def local(x_blocks, columns, filter_ids):
+def dense(x_blocks, columns, filter_ids):
     grp_count = lax.axis_size("grp")
     col_count = lax.axis_size("col")
     rows_a = x_blocks.shape[0]
@@ -108,6 +122,395 @@
     return result.astype(jnp.bfloat16).reshape(x_blocks.shape)
 
 
+def list_codes(columns, filter_ids):
+    grid_a, grid_c, _ = columns.shape
+    chips = grid_a // (2 * RA)
+    ids = (
+        lax.broadcasted_iota(jnp.int32, (grid_a, grid_c), 0) * grid_c
+        + lax.broadcasted_iota(jnp.int32, (grid_a, grid_c), 1)
+    )
+    row_in_chip = lax.broadcasted_iota(jnp.int32, (grid_a, grid_c, 1), 0) % (2 * RA)
+    own, halo = [], []
+    for step_c in (1, -1):
+        found = []
+        for step_a in (-1, 0, 1):
+            cols_r = jnp.roll(columns, (-step_a, -step_c), (0, 1))
+            filt_r = jnp.roll(filter_ids, (-step_a, -step_c), (0, 1))
+            member = jnp.any(cols_r == ids[:, :, None], axis=2)[:, :, None]
+            one = jnp.any(columns[:, :, :, None] == filt_r[:, :, None, :], axis=3) & (columns >= 0)
+            two = jnp.any(filter_ids[:, :, :, None] == cols_r[:, :, None, :], axis=3)
+            found.append((one & member, two & member))
+        up, mid, down = found
+        for phase in (0, 1):
+            first = row_in_chip == 0
+            last = row_in_chip == 2 * RA - 1
+            own.append(mid[phase] | (up[phase] & ~first) | (down[phase] & ~last))
+            halo.append((up[phase] & first) | (down[phase] & last))
+    shape = (2, 2, chips, 2 * RA, grid_c, KB)
+    own = jnp.stack(own).reshape(shape).swapaxes(0, 1)
+    halo = jnp.stack(halo).reshape(shape).swapaxes(0, 1)
+    above = jnp.roll(halo[:, :, :, -1:], 1, axis=2)
+    below = jnp.roll(halo[:, :, :, :1], -1, axis=2)
+    need = jnp.concatenate([above, own, below], axis=3)
+    flags = need.astype(jnp.int32)
+    in_row = jnp.cumsum(flags, axis=5) - flags
+    per_row = flags.sum(axis=5, keepdims=True)
+    row0 = [per_row[:, :, :, i : i + 1] for i in range(CR)]
+    n0 = row0[1] + row0[2] + row0[3] + row0[4]
+    n1 = row0[5] + row0[6] + row0[7] + row0[8]
+    total = n0 + n1 + row0[0] + row0[9]
+    half = (total + 1) // 2
+    base = [n0]
+    run = jnp.zeros_like(n0)
+    for i in range(1, 5):
+        base.append(run)
+        run = run + row0[i]
+    back = jnp.zeros_like(n0)
+    ends = []
+    for i in range(5, 9):
+        ends.append(back)
+        back = back + row0[i]
+    front = jnp.concatenate(base, axis=3) + in_row[:, :, :, 0:5]
+    rear = total - 1 - (jnp.concatenate(ends, axis=3) + in_row[:, :, :, 5:9])
+    last_halo = n0 + row0[0] + in_row[:, :, :, 9:10]
+    place = jnp.concatenate([front, rear, last_halo], axis=3)
+    row = lax.broadcasted_iota(jnp.int32, place.shape, 3)
+    of0 = (row >= 1) & (row <= 4)
+    of1 = (row >= 5) & (row <= 8)
+    slot0 = jnp.where(of0, place, place + jnp.maximum(FIRST - n0, 0))
+    turned = total - 1 - place
+    slot1 = jnp.where(of1, turned, turned + jnp.maximum(FIRST - n1, 0))
+    core = (place >= half).astype(jnp.int32)
+    slot = jnp.where(core == 0, slot0, slot1)
+    most = jnp.max(jnp.where(need, slot + 1, 0), axis=(1, 2, 3, 4, 5))
+    return need, core * 32 + slot, most
+
+
+def tables(columns, filter_ids, need, code, grp, col):
+    grid_a, grid_c, _ = columns.shape
+    z = grp // 2
+    core = grp % 2
+    near_c = jnp.stack([(col - 1) % grid_c, col, (col + 1) % grid_c])
+    chip_need = need[:, :, z]
+    chip_code = code[:, :, z]
+    mine_need = chip_need[:, :, :, col].reshape(2, 2, COLN)
+    mine_code = chip_code[:, :, :, col].reshape(2, 2, COLN)
+    wanted_code = core * 32 + jnp.arange(32, dtype=jnp.int32)
+    hit = mine_need[:, :, None, :] & (mine_code[:, :, None, :] == wanted_code[None, None, :, None])
+    entries = jnp.arange(COLN, dtype=jnp.int32)
+    source = jnp.sum(jnp.where(hit, entries, 0), axis=3)
+    rows_a = (grp * RA - 1 + jnp.arange(RA + 2, dtype=jnp.int32)) % grid_a
+    col_near = columns[rows_a][:, near_c]
+    filt_near = filter_ids[rows_a][:, near_c]
+    row_ids = rows_a[:, None] * grid_c + near_c[None, :]
+    left = lax.dynamic_slice_in_dim(chip_code[:, 0, :, near_c[0]], core * RA, RA + 2, axis=1)
+    right = lax.dynamic_slice_in_dim(chip_code[:, 1, :, near_c[2]], core * RA, RA + 2, axis=1)
+    middle = (core * RA * KB + jnp.arange((RA + 2) * KB, dtype=jnp.int32)).reshape(RA + 2, KB)
+    middle = jnp.broadcast_to(middle, (2, RA + 2, KB))
+    held = jnp.stack([left + 64, middle, right + 128], axis=2)
+    row_cols = col_near[1 : RA + 1, 1]
+    row_filt = filt_near[1 : RA + 1, 1]
+
+    def picks(stored, wanted, where):
+        near = jnp.stack([stored[i : i + 3] for i in range(RA)])
+        spot = jnp.stack([where[i : i + 3] for i in range(RA)])
+        name = jnp.stack([row_ids[i : i + 3] for i in range(RA)])
+        near = near.reshape(RA, 1, 1, 9, 6)
+        spot = spot.reshape(RA, 1, 1, 9, 6)
+        name = name.reshape(RA, 1, 1, 9, 1)
+        same = (row_cols[:, None, :, None, None] == name) & (near == wanted[:, :, None, None, None])
+        return ZERO + jnp.sum(jnp.where(same, spot - ZERO, 0), axis=(3, 4))
+
+    pick1 = picks(col_near, row_filt, held[0])
+    pick2 = picks(filt_near, row_cols, held[1])
+    used = (row_cols >= 0).astype(jnp.int32)
+    parts = [source, pick1, pick2, used]
+    return jnp.concatenate([p.astype(jnp.int32).reshape(-1) for p in parts])
+
+
+def kernel(q1, q2, grp_count, col_count, idx, x_hbm, out_hbm, xv, colp1, rcv1, snd1, colp2, rcv2,
+           snd2, sown, outv, lsem, osem, zsem, hs1, hr1, fs1, fr1, hs2, hr2, fs2, fr2):
+    grp = lax.axis_index("grp")
+    col = lax.axis_index("col")
+    core = lax.rem(grp, 2)
+    partner = (grp + 1 - 2 * core, col)
+    zpeer = (lax.rem(grp + grp_count - 1 + 2 * core, grp_count), col)
+    right = (grp, lax.rem(col + 1, col_count))
+    left = (grp, lax.rem(col + col_count - 1, col_count))
+    own0 = (1 + RA * core) * KB
+    zout = (RA - 1) * core * KB
+    zdst = (CR - 1) * (1 - core) * KB
+    zin = (CR - 1) * core * KB
+
+    to_xv = pltpu.make_async_copy(x_hbm, xv, lsem.at[0])
+    to_col = pltpu.make_async_copy(x_hbm, colp1.at[pl.ds(own0, OWN)], lsem.at[1])
+    to_xv.start()
+    to_col.start()
+
+    barrier = pltpu.get_barrier_semaphore()
+    for peer in (partner, zpeer, right, left):
+        pl.semaphore_signal(barrier, inc=1, device_id=peer, device_id_type=MESH)
+    pl.semaphore_wait(barrier, 4)
+
+    def remote(src, dst, send, recv, device):
+        return pltpu.make_async_remote_copy(
+            src_ref=src, dst_ref=dst, send_sem=send, recv_sem=recv,
+            device_id=device, device_id_type=MESH,
+        )
+
+    def zsend(src, colp, p):
+        return remote(src.at[pl.ds(zout, KB)], colp.at[pl.ds(zdst, KB)],
+                      zsem.at[p, 0], zsem.at[p, 1], zpeer)
+
+    def zfwd(colp, p):
+        here = colp.at[pl.ds(zin, KB)]
+        return remote(here, here, zsem.at[p, 2], zsem.at[p, 3], partner)
+
+    def share(src, colp, p):
+        return remote(src, colp.at[pl.ds(own0, OWN)], zsem.at[p, 4], zsem.at[p, 5], partner)
+
+    def hop(snd, rcv, hs, hr, d, s):
+        return remote(snd.at[d, s], rcv.at[2 * d + core, s], hs.at[d, s], hr.at[d, s],
+                      (right, left)[d])
+
+    def fwd(rcv, fs, fr, d, s):
+        here = rcv.at[2 * d + core, s]
+        return remote(here, here, fs.at[d, s], fr.at[d, s], partner)
+
+    def right_factor(colp, rcv, v):
+        is_col = v < 64
+        at_col = jnp.where(is_col, v, ZERO)
+        at_rcv = jnp.where(is_col, 0, v - 64)
+        return jnp.where(is_col, colp[at_col], rcv[at_rcv >> 5, at_rcv & 31])
+
+    def product(colp, rcv, table, row, entry):
+        acc = None
+        for k in range(KB):
+            v = idx[table + entry * KB + k]
+            term = jnp.dot(xv[row * KB + k], right_factor(colp, rcv, v),
+                           preferred_element_type=jnp.float32)
+            acc = term if acc is None else acc + term
+        return acc
+
+    def list_entry(table, d, s):
+        return jnp.clip(idx[table + d * 32 + s] - own0, 0, OWN - 1)
+
+    zero = jnp.zeros((B, B), jnp.bfloat16)
+
+    to_xv.wait()
+    zs1, zf1, sh1 = zsend(xv, colp1, 0), zfwd(colp1, 0), share(xv, colp1, 0)
+    zs1.start()
+    sh1.start()
+    hop1 = functools.partial(hop, snd1, rcv1, hs1, hr1)
+    fwd1 = functools.partial(fwd, rcv1, fs1, fr1)
+
+    @pl.loop(0, FIRST)
+    def _(s):
+        for d in range(2):
+            snd1[d, s] = xv[list_entry(SRC1, d, s)]
+
+        @pl.when(s > 0)
+        def _():
+            for d in range(2):
+                hop1(d, s - 1).start()
+
+    colp1[ZERO] = zero
+    colp2[ZERO] = zero
+    for d in range(2):
+        hop1(d, FIRST - 1).start()
+    to_col.wait()
+    zs1.wait_recv()
+    zf1.start()
+    sh1.wait_recv()
+    zf1.wait_recv()
+
+    @pl.loop(FIRST, q1)
+    def _(s):
+        for d in range(2):
+            snd1[d, s] = colp1[idx[SRC1 + d * 32 + s]]
+
+        @pl.when(s > FIRST)
+        def _():
+            for d in range(2):
+                hop1(d, s - 1).start()
+
+    for d in range(2):
+        hop1(d, q1 - 1).start()
+
+    @pl.loop(0, q1)
+    def _(s):
+        for d in range(2):
+            hop1(d, s).wait_recv()
+            fwd1(d, s).start()
+
+    @pl.loop(0, q1)
+    def _(s):
+        for d in range(2):
+            fwd1(d, s).wait_recv()
+
+    zs2, zf2, sh2 = zsend(sown, colp2, 1), zfwd(colp2, 1), share(sown, colp2, 1)
+    hop2 = functools.partial(hop, snd2, rcv2, hs2, hr2)
+    fwd2 = functools.partial(fwd, rcv2, fs2, fr2)
+
+    @pl.loop(0, 2)
+    def _(s):
+        for d in range(2):
+            entry = list_entry(SRC2, d, s)
+            snd2[d, s] = product(colp1, rcv1, PICK1, entry // KB, entry).astype(jnp.bfloat16)
+
+        @pl.when(s > 0)
+        def _():
+            for d in range(2):
+                hop2(d, s - 1).start()
+
+    @pl.loop(0, OWN // 2)
+    def _(t):
+        step = t // 3
+        row = step + core * (RA - 1 - 2 * step)
+        for u in range(2):
+            entry = row * KB + (t - 3 * step) * 2 + u
+            block = product(colp1, rcv1, PICK1, row, entry).astype(jnp.bfloat16)
+            sown[entry] = block
+            colp2[own0 + entry] = block
+
+        @pl.when(t == 0)
+        def _():
+            for d in range(2):
+                hop2(d, 1).start()
+
+        @pl.when(t == 3)
+        def _():
+            zs2.start()
+
+    @pl.loop(2, FIRST)
+    def _(s):
+        for d in range(2):
+            snd2[d, s] = sown[list_entry(SRC2, d, s)]
+
+        @pl.when(s > 2)
+        def _():
+            for d in range(2):
+                hop2(d, s - 1).start()
+
+    sh2.start()
+    for d in range(2):
+        hop2(d, FIRST - 1).start()
+    zs2.wait_recv()
+    zf2.start()
+    sh2.wait_recv()
+    zf2.wait_recv()
+
+    @pl.loop(FIRST, q2)
+    def _(s):
+        for d in range(2):
+            snd2[d, s] = colp2[idx[SRC2 + d * 32 + s]]
+
+        @pl.when(s > FIRST)
+        def _():
+            for d in range(2):
+                hop2(d, s - 1).start()
+
+    for d in range(2):
+        hop2(d, q2 - 1).start()
+
+    @pl.loop(0, q2)
+    def _(s):
+        for d in range(2):
+            hop2(d, s).wait_recv()
+            fwd2(d, s).start()
+
+    @pl.loop(0, q2)
+    def _(s):
+        for d in range(2):
+            fwd2(d, s).wait_recv()
+
+    def write(row):
+        rows = pl.ds(row * KB, KB)
+        return pltpu.make_async_copy(outv.at[rows], out_hbm.at[rows], osem.at[row])
+
+    @pl.loop(0, OWN // 2)
+    def _(t):
+        row = t // 3
+        for u in range(2):
+            entry = 2 * t + u
+            cubed = product(colp2, rcv2, PICK2, row, entry)
+            in_use = idx[USED + entry].astype(jnp.float32)
+            own = xv[entry].astype(jnp.float32)
+            outv[entry] = ((1.5 * own - cubed * (0.5 / (KB * B))) * in_use).astype(jnp.bfloat16)
+
+        @pl.when((t > 0) & (t - 3 * row == 0))
+        def _():
+            write(row - 1).start()
+
+    zs1.wait_send()
+    zf1.wait_send()
+    sh1.wait_send()
+    zs2.wait_send()
+    zf2.wait_send()
+    sh2.wait_send()
+
+    @pl.loop(0, q1)
+    def _(s):
+        for d in range(2):
+            hop1(d, s).wait_send()
+            fwd1(d, s).wait_send()
+
+    @pl.loop(0, q2)
+    def _(s):
+        for d in range(2):
+            hop2(d, s).wait_send()
+            fwd2(d, s).wait_send()
+
+    write(RA - 1).start()
+    for row in range(RA):
+        write(row).wait()
+
+
+def sparse(level, x_blocks, index):
+    q1, q2 = LEVELS[level]
+    blocks = x_blocks.reshape(OWN, B, B)
+    vm = lambda *lead: pltpu.VMEM((*lead, B, B), jnp.bfloat16)
+    dma = lambda *lead: pltpu.SemaphoreType.DMA(lead)
+    out = pl.pallas_call(
+        functools.partial(kernel, q1, q2, lax.axis_size("grp"), lax.axis_size("col")),
+        out_shape=jax.ShapeDtypeStruct(blocks.shape, jnp.bfloat16),
+        in_specs=[
+            pl.BlockSpec(memory_space=pltpu.SMEM),
+            pl.BlockSpec(memory_space=pl.ANY),
+        ],
+        out_specs=pl.BlockSpec(memory_space=pl.ANY),
+        scratch_shapes=[
+            vm(OWN), vm(COLN + 1), vm(4, q1), vm(2, q1), vm(COLN + 1), vm(4, q2), vm(2, q2),
+            vm(OWN), vm(OWN),
+            dma(2), dma(RA), dma(2, 6),
+            dma(2, q1), dma(2, q1), dma(2, q1), dma(2, q1),
+            dma(2, q2), dma(2, q2), dma(2, q2), dma(2, q2),
+        ],
+        compiler_params=pltpu.CompilerParams(
+            collective_id=level, has_side_effects=True, vmem_limit_bytes=62 * 1024 * 1024
+        ),
+        name=f"sign_step_{q1}_{q2}",
+    )(index, blocks)
+    return out.reshape(x_blocks.shape)
+
+
+def local(x_blocks, columns, filter_ids):
+    grp = lax.axis_index("grp")
+    col = lax.axis_index("col")
+    need, code, most = list_codes(columns, filter_ids)
+    index = tables(columns, filter_ids, need, code, grp, col)
+    level = jnp.int32(len(LEVELS))
+    for at in reversed(range(len(LEVELS))):
+        fits = (most[0] <= LEVELS[at][0]) & (most[1] <= LEVELS[at][1])
+        level = jnp.where(fits, at, level)
+    branches = [
+        functools.partial(lambda at, x, c, f, i: sparse(at, x, i), at)
+        for at in range(len(LEVELS))
+    ]
+    branches.append(lambda x, c, f, i: dense(x, c, f))
+    return lax.switch(level, branches, x_blocks, columns, filter_ids, index)
+
+
 def solution(mesh):
     return jax.shard_map(
         local,

time: 438 us -> 407 us (0.929)
  other arithmetic: 35.5 us -> 261 us
  waiting for transfers between devices: 183 us -> 0 us
  local copies, waits for them, and re-layouts: 171 us -> 25.7 us
  Pallas kernels: 0 us -> 111 us
  matrix products: 31.9 us -> 0 us
  starting transfers between devices: 14.1 us -> 0 us
    another operation x4 -> x8, other arithmetic: 3.94 us -> 223 us  [the longest x1 223 us: list_codes(): in_row = jnp.cumsum(flags, axis=5) - flags]
    ppermute x8 -> x0, waiting for transfers between devices: 183 us -> none  [the longest x4 178 us: padded(): lax.ppermute(tail, axis, [(i, (i + 1) % count) for i in range(count)])]
    gather x26 -> x6, local copies, waits for them, and re-layouts: 131 us -> 2.45 us  [the longest x3 1.22 us: tables(): col_near = columns[rows_a][:, near_c]]
    pallas_call x0 -> x1, Pallas kernels: none -> 111 us  [sparse(): pl.pallas_call(functools.partial(kernel, q1, q2, lax.axis_size('grp'), la...]
    dot_general x8 -> x0, matrix products: 31.9 us -> none  [one_row(): jnp.einsum('kab,kfbc->fac', left_row, picked, preferred_element_type=jnp....]
    sub x0 -> x5, other arithmetic: none -> 25.2 us  [the longest x1 22.7 us: list_codes(): in_row = jnp.cumsum(flags, axis=5) - flags]
    concatenate x2 -> x1, local copies, waits for them, and re-layouts: 20.7 us -> 0.07 us  [list_codes(): front = jnp.concatenate(base, axis=3) + in_row[:, :, :, 0:5]]
    concatenate x2 -> x10, other arithmetic: 20.6 us -> 0.58 us  [the longest x7 0.29 us: list_codes(): filt_r = jnp.roll(filter_ids, (-step_a, -step_c), (0, 1))]
  transfers between devices with their start and end apart: 8 -> 0, of which waited for: 6 -> 0; matrix products, arithmetic and copies ran while one was open for 3% -> 0% of each run, Pallas kernels for 0% -> 0%
where the time goes in v1:
time: 407 us; the launch traced here: 403 us
  other arithmetic  261 us (64%)
  Pallas kernels  111 us (27%)
  local copies, waits for them, and re-layouts  25.7 us (6%)
    another operation x1, other arithmetic, list_codes(): in_row = jnp.cumsum(flags, axis=5) - flags  223 us
    pallas_call x1, Pallas kernels, sparse(): pl.pallas_call(functools.partial(kernel, q1, q2, lax.axis_size('grp'), la...  111 us
    sub x1, other arithmetic, list_codes(): in_row = jnp.cumsum(flags, axis=5) - flags  22.7 us

profile of v1, /device:TPU:1, one launch (start us, length us, event | category | flops | bytes accessed | tf_op | source)
XLA Modules:
  0.0 402.6 jit_solution(11978597889035691157)
XLA Ops:
  0.0 1.0 fusion.70
  1.0 1.0 fusion.71
  1.9 0.1 pad_add_fusion.5
  2.2 0.9 fusion.68
  3.1 0.8 fusion.69
  3.9 1.0 fusion.66
  4.9 1.0 fusion.67
  5.8 0.1 pad_add_fusion.4
  6.2 0.3 compare_reduce_fusion.5
  6.6 0.3 compare_reduce_fusion.4
  7.0 0.2 copy.590
  7.3 1.1 copy.591
  8.4 0.2 copy.588
  8.6 1.1 copy.589
  9.8 1.1 fusion.61
  10.9 222.5 %reduce_window_sum.11 = s32[2,2,4,10,16,6]{5,0,4,3,2,1:T(2,128)S(1)} reduce-window(s32[2,2,4,10,16,6]{5,0,4,3,2,1:T(2,128)S(1)} %get-tuple-element.318, s32[]{:T(128)} %constant.490.clone.1), window={size=1x1x1x1x1x6 pad=0_0x0_0x0_0x0_0x0_0x5_0}, to_apply=%region_19.20 | reduce-window | flops 76800 | bytes 122884 | tf_op jit(solution)/shard_map/jit(cumsum)/reduce_window_sum | solution.py:156
  233.4 22.7 %convert_subtract_fusion = (s32[2,2,4,10,16,6]{5,0,4,3,2,1:T(2,128)S(1)}, s32[2,2,4,10,16]{0,4,3,2,1:T(8,128)}) fusion(s32[2,2,4,10,16,6]{5,0,4,3,2,1:T(2,128)S(1)} %reduce_window_sum.11, pred[2,2,4,10,16,6]{5,0,4,3,2,1:T(4,128)(4,1)S(1)} %get-tuple-element.319), kind=kLoop, calls=%fused_computation.107 | loop fusion | flops 43520 | bytes 148480 | tf_op jit(solution)/shard_map/sub | solution.py:156
  256.1 2.0 copy.679
  258.3 0.3 copy.593
  258.7 1.0 slice_add_fusion
  259.7 1.0 copy.595
  260.7 0.1 copy.594
  260.8 2.5 fusion.40
  263.3 0.1 copy.600
  263.4 0.8 copy.596
  264.1 1.0 slice_add_fusion.2
  265.2 0.7 copy.597
  265.9 0.7 copy.598
  266.7 4.6 %select_add_fusion = (s32[2,2,4,10,16,6]{5,0,4,3,2,1:T(2,128)}, s32[2,2,4,10,16,6]{5,0,4,3,2,1:T(2,128)S(1)}) fusion(s32[2,2,4,16]{0,3,2,1:T(8,128)} %copy.597, s32[2,2,4,1,16,6]{5,0,4,3,2,1:T(2,128)S(1)} %slice_add_fusion.2, s32[2,2,4,4,16,6]{5,0,4,3,2,1:T(2,128)S(1)} %fusion.40, s32[2,2,4,5,16,6]{5,0,4,3,2,1:T(2,128)S(1)} %slice_add_fusion, ...), kind=kLoop, calls=%fused_computation.103 | loop fusion | flops 199680 | bytes 188436 | tf_op jit(solution)/shard_map/add | solution.py:186
  271.3 0.7 constant_dynamic-slice_fusion
  272.2 0.2 select_reduce_fusion.3
  272.5 0.7 add_bitcast_fusion.4
  274.4 0.6 gather_fusion.6
  275.0 0.1 copy.604
  275.1 0.6 gather_fusion.7
  275.7 0.1 copy.658
  276.6 0.6 gather_fusion.8
  277.2 0.1 copy.615
  277.3 0.6 gather_fusion.9
  277.9 0.1 copy.662
  279.6 1.3 select_reduce_fusion.2
  280.9 0.1 copy.625
  281.2 0.1 copy.643
  281.6 1.5 select_reduce_fusion
  283.1 0.6 fusion.76
  286.3 111.9 %conditional.1 = (bf16[4,1,6,256,256]{4,3,2,1,0:T(8,128)(2,1)}) conditional(s32[]{:T(128)} %bitcast.57, (bf16[4,1,6,256,256]{4,3,2,1,0:T(8,128)(2,1)}, s32[440]{0:T(512)S(1)}) %tuple.25, (bf16[4,1,6,256,256]{4,3,2,1,0:T(8,128)(2,1)}, s32[440]{0:T(512)S(1)}) %tuple.25, (bf16[4,1,6,256,256]{4,3,2,1,0:T(8,128)(2,1)}, ...), branch_computations={%region_24.25_spmd, %region_25.26_spmd, %region_26.35_spmd} | conditional | flops 2497731584 | bytes 335111040 | solution.py:511
  286.4 110.6 %sign_step_13_16.1 = bf16[24,256,256]{2,1,0:T(8,128)(2,1)} custom-call(s32[440]{0:T(512)S(1)} %get-tuple-element.70.idx, bf16[24,256,256]{2,1,0:T(8,128)(2,1)} %bitcast.1.x_hbm), custom_call_target="tpu_custom_call" | custom-call | tf_op jit(solution)/shard_map/cond/branch_0_fun/sign_step_13_16/pallas_call | solution.py:474
  398.2 3.9 copy.712
  (109 shorter events, 5.3 us)
Async XLA Ops:
  0.0 6.2 %copy-start.2 = (s32[32,16,6]{0,1,2:T(8,128)S(1)}, s32[32,16,6]{0,1,2:T(8,128)}, u32[]{:S(2)}) copy-start(s32[32,16,6]{0,1,2:T(8,128)} %param.11) | copy-start | bytes 36868
  0.0 6.1 %copy-start.3 = (s32[32,16,6]{0,1,2:T(8,128)S(1)}, s32[32,16,6]{0,1,2:T(8,128)}, u32[]{:S(2)}) copy-start(s32[32,16,6]{0,1,2:T(8,128)} %param.12) | copy-start | bytes 36868
